TPU v7x, 32 devices: a whole 2x2x4 slice. The times are simulated.
32 devices in a mesh: tile: 8 (over z, y), mem: 4 (over x, core).
Axes of the slice: x: 2, y: 2, z: 4, core: 2. Of those that a mesh axis runs over, the one named last changes fastest.
Arguments:
- background: bfloat16 [112, 80, 512], P('tile', 'mem'), may hold values from -6 to 6
- obs_ens: bfloat16 [112, 80, 128], P('tile', 'mem'), may hold values from -6 to 6
- innovation: float32 [112, 128], P('tile'), may hold values from -6 to 6
- precision: float32 [112, 128], P('tile'), may hold values from 0.1 to 2
- loc_weight: float32 [112, 7], P('tile'), may hold values from 0.1 to 1
- old_split: int32 [9], replicated, may hold values from 0 to 64, as said below
- new_split: int32 [9], replicated, may hold values from 0 to 64, as said below
- obs_count: int32 [112], P('tile'), may hold values from 32 to 128
- halo_tiles: int32 [8, 12], replicated, may hold values from 0 to 63, as said below
- region_list: int32 [112, 7], P('tile'), may hold values from 0 to 25, as said below
Outputs:
- analysis: bfloat16 [112, 80, 512], P('tile', 'mem')
Inputs may be any that keep to these rules, and one draw needn't show every extreme that they name: old_split[0] = 0 and old_split[8] = 64; each device holds between 2 and 14 old tiles, exactly 14 on some device. new_split[0] = 0 and new_split[8] = 64; each device holds between 6 and 10 new tiles; every new_split[d] differs from old_split[d] by at most 2, by exactly 2 for some d. `halo_tiles`: row d is 3 groups of 4 entries; a group holds distinct tiles in rising order that one device p other than d holds under new_split, with p within 3 of d, and the 3 devices of a row are distinct. `region_list`: for a slot of device d, an entry r < 14 names d's slot r, which is live; an entry r >= 14 names the tile halo_tiles[d, r - 14].
All inputs are finite; a program needn't handle non-finite values.
Results may differ from a plain program's by a relative error of at most 0.0057.
Values may be sent and summed in bfloat16 or wider, within the bound.
A program may use at most 64 MiB of HBM per device.

v0:
```python
import math

import jax
import jax.numpy as jnp
from jax import lax
from jax.sharding import PartitionSpec as P

TILE_MEAN = 8
REACH = 3
HPEER = 3
HCAP = 4
NS_ITERS = 6


inflation = 1.1
exact = lax.Precision.HIGHEST


def from_behind(value, axis, steps):
    count = lax.axis_size(axis)
    first, last = (max(0, -steps), min(count, count - steps))
    return lax.ppermute(value, axis, [(source, source + steps) for source in range(first, last)])


def owner_of(split_points, position):
    bounds = split_points[1:]
    return jnp.sum((bounds[None, :] <= position[:, None]).astype(jnp.int32), axis=1)


def pick_slots(wanted, range_start, range_end, capacity):
    leading = wanted[..., 0]
    owned_flag = ((leading >= range_start) & (leading < range_end)).astype(jnp.int32)
    rows_here = jnp.sum(owned_flag[..., None] * (wanted - range_start), axis=-2)
    return jnp.clip(rows_here, 0, capacity - 1)


def inverse_root(system, repeats):
    identity = jnp.eye(system.shape[-1], dtype=system.dtype)
    frobenius = jnp.sqrt(jnp.sum(system * system, axis=(1, 2)))
    root_part = system / frobenius[:, None, None]
    inverse_part = jnp.broadcast_to(identity, system.shape)
    for repeat in range(repeats):
        middle = 0.5 * (
            3.0 * identity - jnp.einsum("pij,pjk->pik", inverse_part, root_part, precision=exact)
        )
        root_part = jnp.einsum("pij,pjk->pik", root_part, middle, precision=exact)
        inverse_part = jnp.einsum("pij,pjk->pik", middle, inverse_part, precision=exact)
    return (inverse_part, frobenius)


def weighted_gram(region, region_pulled, row_weights):
    products = jnp.einsum("pekn,pejn->pekj", region, region, preferred_element_type=jnp.float32)
    gram_matrix = jnp.sum(row_weights[:, :, None, None] * products, axis=1)
    pull_terms = jnp.einsum(
        "pekn,pen->pek", region, region_pulled, preferred_element_type=jnp.float32
    )
    return (gram_matrix, jnp.sum(row_weights[:, :, None] * pull_terms, axis=1))


def shards(
    background,
    obs_ens,
    innovation,
    precision,
    loc_weight,
    old_split,
    new_split,
    obs_count,
    halo_tiles,
    region_list,
):
    capacity = background.shape[0]
    members_here = background.shape[1]
    state_width = background.shape[2]
    obs_slots = obs_ens.shape[2]
    devices = lax.axis_size("tile")
    ensemble = members_here * lax.axis_size("mem")
    myself = lax.axis_index("tile")
    member_rank = lax.axis_index("mem")
    old_start = old_split[myself]
    old_end = old_split[myself + 1]
    new_start = new_split[myself]
    new_end = new_split[myself + 1]
    slot_index = jnp.arange(capacity, dtype=jnp.int32)
    position = new_start + slot_index
    from_left = from_behind(background, "tile", 1)
    from_right = from_behind(background, "tile", -1)
    left_index = position - old_split[jnp.maximum(myself - 1, 0)]
    right_index = 2 * capacity + position - old_end
    combined = jnp.concatenate([from_left, background, from_right], axis=0)
    own_index = capacity + position - old_start
    source = jnp.where(
        position < old_start, left_index, jnp.where(position < old_end, own_index, right_index)
    )
    source = jnp.clip(source, 0, combined.shape[0] - 1)
    migrated = jnp.take(combined, source, axis=0)
    live_obs = (jnp.arange(obs_slots, dtype=jnp.int32)[None, :] < obs_count[:, None]).astype(
        jnp.float32
    )
    root_weight = jnp.sqrt(precision * live_obs)
    scaled = (obs_ens * root_weight[:, None, :]).astype(jnp.bfloat16)
    pulled = (root_weight * innovation).astype(jnp.bfloat16)
    groups = halo_tiles.reshape(devices, HPEER, HCAP)
    mine_groups = groups[myself]
    source_peer = owner_of(new_split, mine_groups[:, 0])
    halo_scaled = jnp.zeros((HPEER, HCAP, members_here, obs_slots), jnp.bfloat16)
    halo_pulled = jnp.zeros((HPEER, HCAP, obs_slots), jnp.bfloat16)
    for offset in list(range(-REACH, 0)) + list(range(1, REACH + 1)):
        reader = jnp.clip(myself - offset, 0, devices - 1)
        chosen_rows = pick_slots(groups[reader], new_start, new_end, capacity)
        arrived = from_behind((scaled[chosen_rows], pulled[chosen_rows]), "tile", -offset)
        matches = source_peer == myself + offset
        halo_scaled = jnp.where(matches[:, None, None, None], arrived[0][None], halo_scaled)
        halo_pulled = jnp.where(matches[:, None, None], arrived[1][None], halo_pulled)
    halo_count = halo_scaled.shape[0] * halo_scaled.shape[1]
    table_scaled = jnp.concatenate(
        [scaled, halo_scaled.reshape(halo_count, members_here, obs_slots)], axis=0
    )
    table_pulled = jnp.concatenate([pulled, halo_pulled.reshape(halo_count, obs_slots)], axis=0)
    full_table = lax.all_gather(table_scaled, "mem", axis=1, tiled=True)
    entries = jnp.concatenate([slot_index[:, None], region_list], axis=1)
    weights = jnp.concatenate([jnp.ones((capacity, 1), jnp.float32), loc_weight], axis=1)
    per_block = capacity * 4 // TILE_MEAN
    live_count = new_end - new_start
    block_count = capacity // per_block
    identity = jnp.eye(ensemble, dtype=jnp.float32)
    column_start = member_rank * members_here

    def analyse(block_index, output):
        first_slot = block_index * per_block
        region_rows = lax.dynamic_slice_in_dim(entries, first_slot, per_block, 0)
        row_weights = lax.dynamic_slice_in_dim(weights, first_slot, per_block, 0)
        region_pulled = table_pulled[region_rows]
        gram_matrix, pull_sum = weighted_gram(full_table[region_rows], region_pulled, row_weights)
        system = gram_matrix + (ensemble - 1) / inflation * identity
        inverse, frobenius = inverse_root(system, NS_ITERS)
        spread = (math.sqrt(ensemble - 1) / jnp.sqrt(frobenius))[:, None, None] * inverse
        half_way = jnp.einsum("pij,pj->pi", inverse, pull_sum, precision=exact)
        mean_weight = (
            jnp.einsum("pij,pj->pi", inverse, half_way, precision=exact) / frobenius[:, None]
        )
        transform = (spread + mean_weight[:, :, None]).astype(jnp.bfloat16)
        columns = lax.dynamic_slice_in_dim(transform, column_start, members_here, 2)
        keep_share = 1.0 - jnp.sum(columns.astype(jnp.float32), axis=1)
        state_block = lax.dynamic_slice_in_dim(migrated, first_slot, per_block, 0)
        member_piece = lax.all_gather(state_block, "mem", axis=1, tiled=True)
        blended = jnp.einsum(
            "pij,pis->pjs", columns, member_piece, preferred_element_type=jnp.float32
        )
        member_total = jnp.sum(member_piece.astype(jnp.float32), axis=1)
        blended, member_total = (blended, member_total)
        mean_state = member_total / ensemble
        analysis_block = blended + keep_share[:, :, None] * mean_state[:, None, :]
        live_rows = (first_slot + jnp.arange(per_block, dtype=jnp.int32) < live_count)[
            :, None, None
        ]
        result = jnp.where(live_rows, analysis_block, 0.0).astype(jnp.bfloat16)
        return lax.dynamic_update_slice_in_dim(output, result, first_slot, 0)

    output = jnp.zeros((capacity, members_here, state_width), jnp.bfloat16)
    return lax.fori_loop(0, block_count, analyse, output)


def solution(mesh):
    in_specs = (
        P("tile", "mem", None),
        P("tile", "mem", None),
        P("tile", None),
        P("tile", None),
        P("tile", None),
        P(),
        P(),
        P("tile"),
        P(),
        P("tile", None),
    )
    out_specs = P("tile", "mem", None)
    return jax.shard_map(shards, mesh=mesh, in_specs=in_specs, out_specs=out_specs, check_vma=False)
```

profile of v0, /device:TPU:0, one launch (start us, length us, event | category | flops | bytes accessed | tf_op | source)
XLA Modules:
  0.0 137.3 jit_solution(18428912862237841192)
XLA Ops:
  0.0 0.8 copy.55
  0.8 1.3 fusion.42
  2.7 1.3 convert_reduce_fusion.7
  4.0 0.6 multiply_reduce_fusion.8
  4.7 1.3 convert_reduce_fusion.6
  6.0 0.6 multiply_reduce_fusion.7
  6.6 0.8 multiply_convert_fusion.1
  7.4 0.6 gather_fusion.8
  8.0 1.3 collective-permute-start.6
  9.3 0.6 gather_fusion.9
  9.9 1.3 collective-permute-start.7
  11.2 1.3 convert_reduce_fusion.4
  12.5 0.6 multiply_reduce_fusion.5
  13.1 1.3 convert_reduce_fusion.5
  14.4 0.6 multiply_reduce_fusion.6
  15.1 0.6 gather_fusion.10
  15.7 1.3 collective-permute-start.8
  17.0 0.6 gather_fusion.11
  17.5 5.5 %collective-permute-start.9 = (bf16[4,128]{1,0:T(4,128)(2,1)S(1)}, bf16[4,128]{1,0:T(4,128)(2,1)S(1)}, u32[]{:S(2)}, u32[]{:S(2)}) collective-permute-start(bf16[4,128]{1,0:T(4,128)(2,1)S(1)} %gather_fusion.11), channel_id=1, source_target_pairs={{0,4},{4,8},{8,12},{12,16},{16,20},{20,24},{24,28},{1,5},{5,9},{9,... | collective-permute-start | bytes 3080 | tf_op jit(solution)/shard_map/ppermute | solution.py:22
  23.1 1.3 convert_reduce_fusion.2
  24.4 0.6 multiply_reduce_fusion.3
  25.0 1.3 convert_reduce_fusion.3
  26.3 0.6 multiply_reduce_fusion.4
  27.0 0.6 gather_fusion.12
  27.5 4.7 %collective-permute-start.10 = (bf16[4,128]{1,0:T(4,128)(2,1)S(1)}, bf16[4,128]{1,0:T(4,128)(2,1)S(1)}, u32[]{:S(2)}, u32[]{:S(2)}) collective-permute-start(bf16[4,128]{1,0:T(4,128)(2,1)S(1)} %gather_fusion.12), channel_id=1, source_target_pairs={{0,8},{4,12},{8,16},{12,20},{16,24},{20,28},{1,9},{5,13},{9,17},{1... | collective-permute-start | bytes 3080 | tf_op jit(solution)/shard_map/ppermute | solution.py:22
  32.3 0.7 slice.24
  34.2 1.4 %fusion.41 = (s32[1]{0:T(128)}, s32[1]{0:T(128)}, s32[1]{0:T(128)}) fusion(s32[9]{0:T(128)} %param.17, s32[]{:T(128)S(6)} %select_n.224, s32[]{:T(128)S(6)} %select_n.223, s32[]{:T(128)S(6)} %max.50), kind=kLoop, calls=%fused_computation.137 | loop fusion | bytes 36 | tf_op jit(solution)/shard_map/dynamic_slice | solution.py:80
  35.6 2.4 %fusion.40 = s32[14]{0:T(128)S(1)} fusion(s32[]{:T(128)} %bitcast.22, s32[]{:T(128)} %bitcast.21, s32[]{:T(128)} %bitcast.20, s32[]{:T(128)} %bitcast.1), kind=kLoop, calls=%fused_computation.130 | loop fusion | flops 196 | bytes 72 | tf_op jit(solution)/shard_map/jit(_take)/jit(_where)/select_n | solution.py:96
  38.1 2.4 %compare_and_fusion = pred[14]{0:T(512)(128)(4,1)S(1)} fusion(s32[]{:T(128)} %bitcast.22, s32[]{:T(128)} %bitcast.21, s32[]{:T(128)} %bitcast.20, s32[]{:T(128)} %bitcast.1), kind=kLoop, calls=%fused_computation.119 | loop fusion | flops 238 | bytes 30 | tf_op jit(solution)/shard_map/jit(_take)/and | solution.py:96
  40.6 0.6 gather_fusion.13
  41.1 0.9 multiply_convert_fusion
  42.0 0.6 gather_fusion.7
  42.6 0.6 gather_fusion.6
  43.2 0.6 gather_fusion.5
  45.4 0.8 copy.52
  46.5 0.8 copy.53
  48.5 6.3 %collective-permute-start.11 = (bf16[4,128]{1,0:T(4,128)(2,1)S(1)}, bf16[4,128]{1,0:T(4,128)(2,1)S(1)}, u32[]{:S(2)}, u32[]{:S(2)}) collective-permute-start(bf16[4,128]{1,0:T(4,128)(2,1)S(1)} %gather_fusion.13), channel_id=1, source_target_pairs={{0,12},{4,16},{8,20},{12,24},{16,28},{1,13},{5,17},{9,21},{13,25},... | collective-permute-start | bytes 3080 | tf_op jit(solution)/shard_map/ppermute | solution.py:22
  54.9 1.3 collective-permute-start
  56.3 1.3 collective-permute-start.1
  57.6 1.3 collective-permute-start.2
  58.9 4.5 %collective-permute-start.3 = (bf16[4,20,128]{2,1,0:T(8,128)(2,1)S(1)}, bf16[4,20,128]{2,1,0:T(8,128)(2,1)S(1)}, u32[]{:S(2)}, u32[]{:S(2)}) collective-permute-start(bf16[4,20,128]{2,1,0:T(8,128)(2,1)S(1)} %gather_fusion.5), channel_id=1, source_target_pairs={{0,4},{4,8},{8,12},{12,16},{16,20},{20,24},{24,28},{1,5},{5,9},{9,... | collective-permute-start | bytes 61448 | tf_op jit(solution)/shard_map/ppermute | solution.py:22
  63.5 4.6 %collective-permute-start.4 = (bf16[4,20,128]{2,1,0:T(8,128)(2,1)S(1)}, bf16[4,20,128]{2,1,0:T(8,128)(2,1)S(1)}, u32[]{:S(2)}, u32[]{:S(2)}) collective-permute-start(bf16[4,20,128]{2,1,0:T(8,128)(2,1)S(1)} %gather_fusion.6), channel_id=1, source_target_pairs={{0,8},{4,12},{8,16},{12,20},{16,24},{20,28},{1,9},{5,13},{9,17},{1... | collective-permute-start | bytes 61448 | tf_op jit(solution)/shard_map/ppermute | solution.py:22
  68.3 6.3 %collective-permute-start.5 = (bf16[4,20,128]{2,1,0:T(8,128)(2,1)S(1)}, bf16[4,20,128]{2,1,0:T(8,128)(2,1)S(1)}, u32[]{:S(2)}, u32[]{:S(2)}) collective-permute-start(bf16[4,20,128]{2,1,0:T(8,128)(2,1)S(1)} %gather_fusion.7), channel_id=1, source_target_pairs={{0,12},{4,16},{8,20},{12,24},{16,28},{1,13},{5,17},{9,21},{13,25},... | collective-permute-start | bytes 61448 | tf_op jit(solution)/shard_map/ppermute | solution.py:22
  74.6 1.3 collective-permute-start.13
  75.9 4.6 %collective-permute-start.12 = (bf16[14,20,512]{2,1,0:T(8,128)(2,1)S(1)}, bf16[14,20,512]{2,1,0:T(8,128)(2,1)S(1)}, u32[]{:S(2)}, u32[]{:S(2)}) collective-permute-start(bf16[14,20,512]{2,1,0:T(8,128)(2,1)S(1)} %copy.57), channel_id=1, source_target_pairs={{0,4},{4,8},{8,12},{12,16},{16,20},{20,24},{24,28},{1,5},{5,9},{9,... | collective-permute-start | bytes 860168 | tf_op jit(solution)/shard_map/ppermute | solution.py:22
  80.7 8.4 %all_gather.12 = bf16[26,80,128]{2,0,1:T(8,128)(2,1)S(1)} all-gather(bf16[26,20,128]{2,0,1:T(8,128)(2,1)S(1)} %copy.56), channel_id=1, replica_groups=mesh['tile'=8,'mem'=4] {'mem'}, dimensions={1}, use_global_device_ids=true | all-gather | bytes 665600 | tf_op jit(solution)/shard_map/all_gather | solution.py:120
  89.4 1.2 collective-permute-done.12
  90.7 0.6 gather_fusion.14
  91.6 45.0 %while.16 = (s32[]{:T(128)}, bf16[14,20,512]{2,0,1:T(8,128)(2,1)S(1)}, s32[]{:T(128)}, f32[14,8]{1,0:T(8,128)S(1)}, s32[14,8]{1,0:T(8,128)S(1)}, /*index=5*/bf16...) while((s32[]{:T(128)}, ...), condition=%wide.region_13.14_spmd.clone, body=%wide.region_7.13_spmd.clone.sunk | while | flops 839092416 | bytes 17701984 | solution.py:161
  91.7 0.6 gather_fusion.1
  92.4 7.9 %all_gather.15 = bf16[7,80,512]{2,0,1:T(8,128)(2,1)S(1)} all-gather(bf16[7,20,512]{2,0,1:T(8,128)(2,1)S(1)} %constant_dynamic-slice_fusion.4), channel_id=1, replica_groups=mesh['tile'=8,'mem'=4] {'mem'}, dimensions={1}, use_global_device_ids=true | all-gather | bytes 716800 | tf_op jit(solution)/shard_map/while/body/eval_jaxpr/all_gather | solution.py:146
  100.5 0.8 gather_fusion
  101.3 0.7 fusion.213
  102.0 0.8 multiply_reduce_fusion.12
  109.9 0.6 fusion.212
  111.9 2.1 %dynamic_update_slice.11 = bf16[14,20,512]{2,0,1:T(8,128)(2,1)S(1)} dynamic-update-slice(bf16[14,20,512]{2,0,1:T(8,128)(2,1)S(1)} %get-tuple-element.413, bf16[7,20,512]{2,0,1:T(8,128)(2,1)S(1)} %copy.97, s32[]{:T(128)S(6)} %select_n.351, s32[]{:T(128)} %constant.170.clone.1..sunk, s32[]{:T(128)} %constant.170.clone.1..sunk) | dynamic-update-slice | bytes 286724 | tf_op jit(solution)/shard_map/while/body/eval_jaxpr/dynamic_update_slice | solution.py:158
  114.2 0.6 gather_fusion.1
  114.9 8.0 %all_gather.15 = bf16[7,80,512]{2,0,1:T(8,128)(2,1)S(1)} all-gather(bf16[7,20,512]{2,0,1:T(8,128)(2,1)S(1)} %constant_dynamic-slice_fusion.4), channel_id=1, replica_groups=mesh['tile'=8,'mem'=4] {'mem'}, dimensions={1}, use_global_device_ids=true | all-gather | bytes 716800 | tf_op jit(solution)/shard_map/while/body/eval_jaxpr/all_gather | solution.py:146
  123.1 0.8 gather_fusion
  123.9 0.7 fusion.213
  124.5 0.8 multiply_reduce_fusion.12
  132.4 0.6 fusion.212
  134.5 2.1 %dynamic_update_slice.11 = bf16[14,20,512]{2,0,1:T(8,128)(2,1)S(1)} dynamic-update-slice(bf16[14,20,512]{2,0,1:T(8,128)(2,1)S(1)} %get-tuple-element.413, bf16[7,20,512]{2,0,1:T(8,128)(2,1)S(1)} %copy.97, s32[]{:T(128)S(6)} %select_n.351, s32[]{:T(128)} %constant.170.clone.1..sunk, s32[]{:T(128)} %constant.170.clone.1..sunk) | dynamic-update-slice | bytes 286724 | tf_op jit(solution)/shard_map/while/body/eval_jaxpr/dynamic_update_slice | solution.py:158
  136.6 0.7 copy-done.1
  (146 shorter events, 22.4 us)
Async XLA Ops:
  0.0 48.4 %copy-start = (bf16[14,20,512]{2,0,1:T(8,128)(2,1)S(1)}, bf16[14,20,512]{2,0,1:T(8,128)(2,1)}, u32[]{:S(2)}) copy-start(bf16[14,20,512]{2,0,1:T(8,128)(2,1)} %param.12) | copy-start | bytes 860164
  8.0 40.5 %collective-permute-start.6 = (bf16[4,128]{1,0:T(4,128)(2,1)S(1)}, bf16[4,128]{1,0:T(4,128)(2,1)S(1)}, u32[]{:S(2)}, u32[]{:S(2)}) collective-permute-start(bf16[4,128]{1,0:T(4,128)(2,1)S(1)} %gather_fusion.8), channel_id=1, source_target_pairs={{12,0},{16,4},{20,8},{24,12},{28,16},{13,1},{17,5},{21,9},{25,13},... | collective-permute-start | bytes 3080 | tf_op jit(solution)/shard_map/ppermute | solution.py:22
  9.9 45.1 %collective-permute-start.7 = (bf16[4,128]{1,0:T(4,128)(2,1)S(1)}, bf16[4,128]{1,0:T(4,128)(2,1)S(1)}, u32[]{:S(2)}, u32[]{:S(2)}) collective-permute-start(bf16[4,128]{1,0:T(4,128)(2,1)S(1)} %gather_fusion.9), channel_id=1, source_target_pairs={{8,0},{12,4},{16,8},{20,12},{24,16},{28,20},{9,1},{13,5},{17,9},{2... | collective-permute-start | bytes 3080 | tf_op jit(solution)/shard_map/ppermute | solution.py:22
  15.7 40.6 %collective-permute-start.8 = (bf16[4,128]{1,0:T(4,128)(2,1)S(1)}, bf16[4,128]{1,0:T(4,128)(2,1)S(1)}, u32[]{:S(2)}, u32[]{:S(2)}) collective-permute-start(bf16[4,128]{1,0:T(4,128)(2,1)S(1)} %gather_fusion.10), channel_id=1, source_target_pairs={{4,0},{8,4},{12,8},{16,12},{20,16},{24,20},{28,24},{5,1},{9,5},{13... | collective-permute-start | bytes 3080 | tf_op jit(solution)/shard_map/ppermute | solution.py:22
  17.5 40.1 %collective-permute-start.9 = (bf16[4,128]{1,0:T(4,128)(2,1)S(1)}, bf16[4,128]{1,0:T(4,128)(2,1)S(1)}, u32[]{:S(2)}, u32[]{:S(2)}) collective-permute-start(bf16[4,128]{1,0:T(4,128)(2,1)S(1)} %gather_fusion.11), channel_id=1, source_target_pairs={{0,4},{4,8},{8,12},{12,16},{16,20},{20,24},{24,28},{1,5},{5,9},{9,... | collective-permute-start | bytes 3080 | tf_op jit(solution)/shard_map/ppermute | solution.py:22
  27.5 31.4 %collective-permute-start.10 = (bf16[4,128]{1,0:T(4,128)(2,1)S(1)}, bf16[4,128]{1,0:T(4,128)(2,1)S(1)}, u32[]{:S(2)}, u32[]{:S(2)}) collective-permute-start(bf16[4,128]{1,0:T(4,128)(2,1)S(1)} %gather_fusion.12), channel_id=1, source_target_pairs={{0,8},{4,12},{8,16},{12,20},{16,24},{20,28},{1,9},{5,13},{9,17},{1... | collective-permute-start | bytes 3080 | tf_op jit(solution)/shard_map/ppermute | solution.py:22
  48.5 15.0 %collective-permute-start.11 = (bf16[4,128]{1,0:T(4,128)(2,1)S(1)}, bf16[4,128]{1,0:T(4,128)(2,1)S(1)}, u32[]{:S(2)}, u32[]{:S(2)}) collective-permute-start(bf16[4,128]{1,0:T(4,128)(2,1)S(1)} %gather_fusion.13), channel_id=1, source_target_pairs={{0,12},{4,16},{8,20},{12,24},{16,28},{1,13},{5,17},{9,21},{13,25},... | collective-permute-start | bytes 3080 | tf_op jit(solution)/shard_map/ppermute | solution.py:22
  54.9 13.4 %collective-permute-start = (bf16[4,20,128]{2,1,0:T(8,128)(2,1)S(1)}, bf16[4,20,128]{2,1,0:T(8,128)(2,1)S(1)}, u32[]{:S(2)}, u32[]{:S(2)}) collective-permute-start(bf16[4,20,128]{2,1,0:T(8,128)(2,1)S(1)} %gather_fusion.2), channel_id=1, source_target_pairs={{12,0},{16,4},{20,8},{24,12},{28,16},{13,1},{17,5},{21,9},{25,13},... | collective-permute-start | bytes 61448 | tf_op jit(solution)/shard_map/ppermute | solution.py:22
  56.3 18.3 %collective-permute-start.1 = (bf16[4,20,128]{2,1,0:T(8,128)(2,1)S(1)}, bf16[4,20,128]{2,1,0:T(8,128)(2,1)S(1)}, u32[]{:S(2)}, u32[]{:S(2)}) collective-permute-start(bf16[4,20,128]{2,1,0:T(8,128)(2,1)S(1)} %gather_fusion.3), channel_id=1, source_target_pairs={{8,0},{12,4},{16,8},{20,12},{24,16},{28,20},{9,1},{13,5},{17,9},{2... | collective-permute-start | bytes 61448 | tf_op jit(solution)/shard_map/ppermute | solution.py:22
  57.6 18.3 %collective-permute-start.2 = (bf16[4,20,128]{2,1,0:T(8,128)(2,1)S(1)}, bf16[4,20,128]{2,1,0:T(8,128)(2,1)S(1)}, u32[]{:S(2)}, u32[]{:S(2)}) collective-permute-start(bf16[4,20,128]{2,1,0:T(8,128)(2,1)S(1)} %gather_fusion.4), channel_id=1, source_target_pairs={{4,0},{8,4},{12,8},{16,12},{20,16},{24,20},{28,24},{5,1},{9,5},{13... | collective-permute-start | bytes 61448 | tf_op jit(solution)/shard_map/ppermute | solution.py:22
  58.9 21.6 %collective-permute-start.3 = (bf16[4,20,128]{2,1,0:T(8,128)(2,1)S(1)}, bf16[4,20,128]{2,1,0:T(8,128)(2,1)S(1)}, u32[]{:S(2)}, u32[]{:S(2)}) collective-permute-start(bf16[4,20,128]{2,1,0:T(8,128)(2,1)S(1)} %gather_fusion.5), channel_id=1, source_target_pairs={{0,4},{4,8},{8,12},{12,16},{16,20},{20,24},{24,28},{1,5},{5,9},{9,... | collective-permute-start | bytes 61448 | tf_op jit(solution)/shard_map/ppermute | solution.py:22
  63.5 17.0 %collective-permute-start.4 = (bf16[4,20,128]{2,1,0:T(8,128)(2,1)S(1)}, bf16[4,20,128]{2,1,0:T(8,128)(2,1)S(1)}, u32[]{:S(2)}, u32[]{:S(2)}) collective-permute-start(bf16[4,20,128]{2,1,0:T(8,128)(2,1)S(1)} %gather_fusion.6), channel_id=1, source_target_pairs={{0,8},{4,12},{8,16},{12,20},{16,24},{20,28},{1,9},{5,13},{9,17},{1... | collective-permute-start | bytes 61448 | tf_op jit(solution)/shard_map/ppermute | solution.py:22
  68.3 12.2 %collective-permute-start.5 = (bf16[4,20,128]{2,1,0:T(8,128)(2,1)S(1)}, bf16[4,20,128]{2,1,0:T(8,128)(2,1)S(1)}, u32[]{:S(2)}, u32[]{:S(2)}) collective-permute-start(bf16[4,20,128]{2,1,0:T(8,128)(2,1)S(1)} %gather_fusion.7), channel_id=1, source_target_pairs={{0,12},{4,16},{8,20},{12,24},{16,28},{1,13},{5,17},{9,21},{13,25},... | collective-permute-start | bytes 61448 | tf_op jit(solution)/shard_map/ppermute | solution.py:22
  74.6 14.8 %collective-permute-start.13 = (bf16[14,20,512]{2,1,0:T(8,128)(2,1)S(1)}, bf16[14,20,512]{2,1,0:T(8,128)(2,1)S(1)}, u32[]{:S(2)}, u32[]{:S(2)}) collective-permute-start(bf16[14,20,512]{2,1,0:T(8,128)(2,1)S(1)} %copy.57), channel_id=1, source_target_pairs={{4,0},{8,4},{12,8},{16,12},{20,16},{24,20},{28,24},{5,1},{9,5},{13... | collective-permute-start | bytes 860168 | tf_op jit(solution)/shard_map/ppermute | solution.py:22
  75.9 14.7 %collective-permute-start.12 = (bf16[14,20,512]{2,1,0:T(8,128)(2,1)S(1)}, bf16[14,20,512]{2,1,0:T(8,128)(2,1)S(1)}, u32[]{:S(2)}, u32[]{:S(2)}) collective-permute-start(bf16[14,20,512]{2,1,0:T(8,128)(2,1)S(1)} %copy.57), channel_id=1, source_target_pairs={{0,4},{4,8},{8,12},{12,16},{16,20},{20,24},{24,28},{1,5},{5,9},{9,... | collective-permute-start | bytes 860168 | tf_op jit(solution)/shard_map/ppermute | solution.py:22
  136.6 0.7 copy-start.1
where the time goes:
time: 138 us; the launch traced here: 137 us
  starting transfers between devices  45.6 us (33%)
  blocking collectives  24.3 us (18%)
  local copies, waits for them, and re-layouts  23.7 us (17%)
  other arithmetic  20.6 us (15%)
  matrix products  19.8 us (14%)
  between operations  1.64 us (1%)
    ppermute x14, starting transfers between devices, from_behind(): lax.ppermute(value, axis, [(source, source + steps) for source in range(f...  45.6 us
    all_gather x2, blocking collectives, analyse(): member_piece = lax.all_gather(state_block, 'mem', axis=1, tiled=True)  15.9 us
    all_gather x1, blocking collectives, shards(): full_table = lax.all_gather(table_scaled, 'mem', axis=1, tiled=True)  8.45 us
    mul x6, other arithmetic, pick_slots(): rows_here = jnp.sum(owned_flag[..., None] * (wanted - range_start), axis=-2)  7.84 us
    dot_general x12, matrix products, inverse_root(): jnp.einsum('pij,pjk->pik', middle, inverse_part, precision=exact)  5.39 us
    dot_general x12, matrix products, inverse_root(): jnp.einsum('pij,pjk->pik', inverse_part, root_part, precision=exact)  5.12 us
    dynamic_update_slice x4, local copies, waits for them, and re-layouts, analyse(): return lax.dynamic_update_slice_in_dim(output, result, first_slot, 0)  4.29 us
    dot_general x10, matrix products, inverse_root(): root_part = jnp.einsum('pij,pjk->pik', root_part, middle, precision=exact)  4.28 us
  transfers between devices with their start and end apart: 14, of which 1 were waited for; matrix products, arithmetic and copies ran while one was open for 19% of the time, Pallas kernels for 0%

commit v1 on v0

v1 whole, which is shorter than its diff:
```python
import functools
import math

import jax
import jax.numpy as jnp
from jax import lax
from jax.experimental import pallas as pl
from jax.experimental.pallas import tpu as pltpu
from jax.sharding import PartitionSpec as P

TILE_MEAN = 8
MOVE = 2
REACH = 3
HPEER = 3
HCAP = 4
NS_ITERS = 6
LIVE_MAX = TILE_MEAN + MOVE
INFLATION = 1.1
PAD = 32
MESH = pl.DeviceIdType.MESH
F32 = jnp.float32
BF16 = jnp.bfloat16
OFFSETS = tuple(range(-REACH, 0)) + tuple(range(1, REACH + 1))


def dot(a, b):
    return jnp.dot(a, b, preferred_element_type=F32)


def cut(a):
    high = a.astype(BF16)
    return high, (a - high.astype(F32)).astype(BF16)


def dot3(a, b):
    ah, al = a
    bh, bl = b
    return dot(ah, bh) + (dot(ah, bl) + dot(al, bh))


def kernel(
    devices,
    ranks,
    old_ref,
    new_ref,
    count_ref,
    halo_ref,
    region_ref,
    weight_ref,
    back_ref,
    obs_ref,
    innov_ref,
    prec_ref,
    out_ref,
    mine,
    table,
    stage,
    arrived,
    mig_out,
    mig_in,
    states,
    gram_s,
    y_s,
    z_s,
    t_out,
    t_in,
    halo_send,
    halo_recv,
    mig_send,
    mig_recv,
    own_send,
    own_recv,
    far_send,
    far_recv,
    state_send,
    state_recv,
    t_send,
    t_recv,
):
    capacity, members, width = back_ref.shape
    obs_slots = obs_ref.shape[2]
    ensemble = members * ranks
    full = PAD * ranks
    halo_count = HPEER * HCAP
    per_rank = -(-LIVE_MAX // ranks)
    me = lax.axis_index("tile")
    rank = lax.axis_index("mem")
    peers = [lax.rem(rank + j, ranks) for j in range(1, ranks)]

    barrier = pltpu.get_barrier_semaphore()
    for offset in OFFSETS:
        target = me + offset

        @pl.when((target >= 0) & (target < devices))
        def _():
            pl.semaphore_signal(barrier, inc=1, device_id=(target, rank), device_id_type=MESH)

    for peer in peers:
        pl.semaphore_signal(barrier, inc=1, device_id=(me, peer), device_id_type=MESH)

    old_start, old_end = old_ref[me], old_ref[me + 1]
    new_start, new_end = new_ref[me], new_ref[me + 1]
    row_id = lax.broadcasted_iota(jnp.int32, (PAD, obs_slots), 0)
    lane_id = lax.broadcasted_iota(jnp.int32, (1, obs_slots), 1)

    for s in range(LIVE_MAX):
        live = (lane_id < count_ref[s]).astype(F32)
        root = jnp.sqrt(prec_ref[s : s + 1, :] * live)
        pulled = root * innov_ref[s : s + 1, :]
        rows = obs_ref[s].astype(F32) * root
        fill = jnp.zeros((PAD - members, obs_slots), F32)
        block = jnp.concatenate([rows, fill], axis=0)
        block = jnp.where(row_id == members, pulled, block).astype(BF16)
        mine[s] = block
        table[s, rank] = block

    for k, offset in enumerate(OFFSETS):
        reader = jnp.clip(me + offset, 0, devices - 1)
        for c in range(HCAP):
            index = jnp.int32(0)
            for g in range(HPEER):
                first = halo_ref[reader, g * HCAP]
                here = (first >= new_start) & (first < new_end)
                index += jnp.where(here, halo_ref[reader, g * HCAP + c] - new_start, 0)
            index = jnp.clip(index, 0, LIVE_MAX - 1)
            stage[k, c] = mine[index]

    old_count = old_end - old_start
    for c in range(MOVE):
        mig_out[0, c] = back_ref[jnp.clip(c, 0, capacity - 1)]
        mig_out[1, c] = back_ref[jnp.clip(old_count - MOVE + c, 0, capacity - 1)]
    for s in range(LIVE_MAX):
        states[s, rank] = jnp.zeros((PAD, width), BF16)

    signals = ranks - 1
    for offset in OFFSETS:
        inside = (me + offset >= 0) & (me + offset < devices)
        signals += jnp.where(inside, 1, 0)
    pl.semaphore_wait(barrier, signals)

    def remote(src, dst, send, recv, target):
        return pltpu.make_async_remote_copy(
            src_ref=src,
            dst_ref=dst,
            send_sem=send,
            recv_sem=recv,
            device_id=target,
            device_id_type=MESH,
        )

    halo_copies = []
    for k, offset in enumerate(OFFSETS):
        target = me + offset
        back_slot = len(OFFSETS) - 1 - k
        copy = remote(
            stage.at[k], arrived.at[back_slot], halo_send.at[k], halo_recv.at[back_slot],
            (target, rank),
        )
        source = me + OFFSETS[back_slot]
        halo_copies.append(copy)

        @pl.when((target >= 0) & (target < devices))
        def _(copy=copy):
            copy.start()

    mig_copies = []
    for side, offset in ((0, -1), (1, 1)):
        target = me + offset
        copy = remote(
            mig_out.at[side], mig_in.at[1 - side], mig_send.at[side], mig_recv.at[1 - side],
            (target, rank),
        )
        mig_copies.append(copy)

        @pl.when((target >= 0) & (target < devices))
        def _(copy=copy):
            copy.start()

    own_rows = pl.ds(0, LIVE_MAX)
    far_rows = pl.ds(LIVE_MAX, halo_count)
    own_copies, far_copies, state_copies = [], [], []
    for j, peer in enumerate(peers):
        own = table.at[own_rows, rank]
        own_copies.append(remote(own, own, own_send.at[j], own_recv.at[j], (me, peer)))
        far = table.at[far_rows, rank]
        far_copies.append(remote(far, far, far_send.at[j], far_recv.at[j], (me, peer)))
        piece = states.at[:, rank]
        state_copies.append(remote(piece, piece, state_send.at[j], state_recv.at[j], (me, peer)))
    for copy in own_copies:
        copy.start()

    for k, offset in enumerate(OFFSETS):
        back_slot = len(OFFSETS) - 1 - k
        source = me + OFFSETS[back_slot]

        @pl.when((source >= 0) & (source < devices))
        def _(copy=halo_copies[k]):
            copy.wait_recv()

    for g in range(HPEER):
        first = halo_ref[me, g * HCAP]
        owner = jnp.int32(0)
        for k, offset in enumerate(OFFSETS):
            source = jnp.clip(me + offset, 0, devices - 1)
            held = (first >= new_ref[source]) & (first < new_ref[source + 1])
            inside = (me + offset >= 0) & (me + offset < devices)
            owner = jnp.where(held & inside, k, owner)
        for c in range(HCAP):
            table[LIVE_MAX + g * HCAP + c, rank] = arrived[owner, c]
    for copy in far_copies:
        copy.start()

    for side, offset in ((0, -1), (1, 1)):
        source = me - offset

        @pl.when((source >= 0) & (source < devices))
        def _(copy=mig_copies[side]):
            copy.wait_recv()

    for s in range(LIVE_MAX):
        position = new_start + s
        left = mig_in[0, jnp.clip(position - old_start + MOVE, 0, MOVE - 1)]
        own = back_ref[jnp.clip(position - old_start, 0, capacity - 1)]
        right = mig_in[1, jnp.clip(position - old_end, 0, MOVE - 1)]
        row = jnp.where(position < old_start, left, jnp.where(position < old_end, own, right))
        states[s, rank, :members] = row
    for copy in state_copies:
        copy.start()

    for copy in own_copies:
        copy.wait_recv()
    for copy in far_copies:
        copy.wait_recv()

    grid_row = lax.broadcasted_iota(jnp.int32, (full, full), 0)
    grid_col = lax.broadcasted_iota(jnp.int32, (full, full), 1)
    live_row = lax.rem(grid_row, PAD) < members
    live_col = lax.rem(grid_col, PAD) < members
    unit = (grid_row == grid_col).astype(F32)
    live_unit = jnp.where(live_row, unit, 0.0)
    line = lax.broadcasted_iota(jnp.int32, (1, full), 1)
    live_line = lax.rem(line, PAD) < members
    shift = (ensemble - 1) / INFLATION
    entries = region_ref.shape[1] + 1

    norms, pulls = [], []
    for b in range(per_rank):
        slot = jnp.minimum(rank + b * ranks, LIVE_MAX - 1)
        gram = jnp.zeros((full, full), F32)
        for e in range(entries):
            if e == 0:
                index = slot
            else:
                named = region_ref[slot, e - 1]
                index = jnp.where(named < capacity, named, named - capacity + LIVE_MAX)
            index = jnp.clip(index, 0, LIVE_MAX + halo_count - 1)
            block = table[index].reshape(full, obs_slots)
            product = lax.dot_general(
                block, block, (((1,), (1,)), ((), ())), preferred_element_type=F32
            )
            gram += product if e == 0 else weight_ref[slot, e - 1] * product
        pulls.append(jnp.where(live_line, gram[members : members + 1, :], 0.0))
        system = jnp.where(live_row & live_col, gram, 0.0) + shift * live_unit
        total = jnp.sum(jnp.sum(system * system, axis=1, keepdims=True), axis=0, keepdims=True)
        norm = jnp.sqrt(total)
        norms.append(norm)
        y = system / norm
        middle = 1.5 * unit - 0.5 * y
        y_s[b] = dot3(cut(y), cut(middle))
        z_s[b] = middle

    def step(_, carry):
        middles = []
        for b in range(per_rank):
            middles.append(cut(1.5 * unit - 0.5 * dot3(cut(z_s[b]), cut(y_s[b]))))
        for b in range(per_rank):
            y_s[b] = dot3(cut(y_s[b]), middles[b])
            z_s[b] = dot3(middles[b], cut(z_s[b]))
        return carry

    lax.fori_loop(0, NS_ITERS - 2, step, 0)
    for b in range(per_rank):
        z = cut(z_s[b])
        middle = cut(1.5 * unit - 0.5 * dot3(z, cut(y_s[b])))
        inverse = dot3(middle, z)
        parts = cut(inverse)
        pull = jnp.broadcast_to(pulls[b], (8, full))
        half = dot3(cut(pull), parts)
        shift_row = dot3(cut(half), parts)[:1] / norms[b]
        spread = math.sqrt(ensemble - 1) * lax.rsqrt(norms[b])
        transposed = spread * inverse + jnp.where(live_line, shift_row, 0.0)
        t_out[b] = transposed.astype(BF16).reshape(ranks, PAD, full)

    t_copies = []
    for j, peer in enumerate(peers):
        copy = remote(
            t_out.at[:, peer], t_in.at[rank], t_send.at[j], t_recv.at[j], (me, peer)
        )
        t_copies.append(copy)
        copy.start()
    t_in[rank] = t_out[:, rank]

    for copy in state_copies:
        copy.wait_recv()
    for copy in t_copies:
        copy.wait_recv()

    piece_row = lax.broadcasted_iota(jnp.int32, (PAD, full), 0)
    for s in range(LIVE_MAX):
        weights = t_in[s % ranks, s // ranks]
        weights = jnp.where(piece_row == members, jnp.ones_like(weights), weights)
        keep = 1.0 - jnp.sum(weights.astype(F32), axis=1, keepdims=True)
        blended = dot(weights, states[s].reshape(full, width))
        mean = blended[members : members + 1, :] / ensemble
        value = (blended + keep * mean)[:members]
        is_live = new_start + s < new_end
        out_ref[s] = jnp.where(is_live, value, 0.0).astype(BF16)
    for s in range(LIVE_MAX, capacity):
        out_ref[s] = jnp.zeros((members, width), BF16)

    for k, offset in enumerate(OFFSETS):
        target = me + offset

        @pl.when((target >= 0) & (target < devices))
        def _(copy=halo_copies[k]):
            copy.wait_send()

    for side, offset in ((0, -1), (1, 1)):
        target = me + offset

        @pl.when((target >= 0) & (target < devices))
        def _(copy=mig_copies[side]):
            copy.wait_send()

    for copy in own_copies + far_copies + state_copies + t_copies:
        copy.wait_send()


def shards(devices, ranks, background, obs_ens, innovation, precision, loc_weight, old_split,
           new_split, obs_count, halo_tiles, region_list):
    capacity, members, width = background.shape
    obs_slots = obs_ens.shape[2]
    full = PAD * ranks
    halo_count = HPEER * HCAP
    per_rank = -(-LIVE_MAX // ranks)
    smem = pl.BlockSpec(memory_space=pltpu.SMEM)
    vmem = pl.BlockSpec(memory_space=pltpu.VMEM)
    count = len(OFFSETS)
    dma = pltpu.SemaphoreType.DMA
    return pl.pallas_call(
        functools.partial(kernel, devices, ranks),
        out_shape=jax.ShapeDtypeStruct((capacity, members, width), BF16),
        in_specs=[smem] * 6 + [vmem] * 4,
        out_specs=vmem,
        scratch_shapes=[
            pltpu.VMEM((LIVE_MAX, PAD, obs_slots), BF16),
            pltpu.VMEM((LIVE_MAX + halo_count, ranks, PAD, obs_slots), BF16),
            pltpu.VMEM((count, HCAP, PAD, obs_slots), BF16),
            pltpu.VMEM((count, HCAP, PAD, obs_slots), BF16),
            pltpu.VMEM((2, MOVE, members, width), BF16),
            pltpu.VMEM((2, MOVE, members, width), BF16),
            pltpu.VMEM((LIVE_MAX, ranks, PAD, width), BF16),
            pltpu.VMEM((per_rank, full, full), F32),
            pltpu.VMEM((per_rank, full, full), F32),
            pltpu.VMEM((per_rank, full, full), F32),
            pltpu.VMEM((per_rank, ranks, PAD, full), BF16),
            pltpu.VMEM((ranks, per_rank, PAD, full), BF16),
            dma((count,)),
            dma((count,)),
            dma((2,)),
            dma((2,)),
            dma((ranks - 1,)),
            dma((ranks - 1,)),
            dma((ranks - 1,)),
            dma((ranks - 1,)),
            dma((ranks - 1,)),
            dma((ranks - 1,)),
            dma((ranks - 1,)),
            dma((ranks - 1,)),
        ],
        compiler_params=pltpu.CompilerParams(collective_id=0, has_side_effects=True),
        cost_estimate=pl.CostEstimate(flops=10**8, bytes_accessed=10**7, transcendentals=0),
    )(old_split, new_split, obs_count, halo_tiles, region_list, loc_weight, background, obs_ens,
      innovation, precision)


def solution(mesh):
    in_specs = (
        P("tile", "mem", None),
        P("tile", "mem", None),
        P("tile", None),
        P("tile", None),
        P("tile", None),
        P(),
        P(),
        P("tile"),
        P(),
        P("tile", None),
    )
    out_specs = P("tile", "mem", None)
    body = functools.partial(shards, mesh.shape["tile"], mesh.shape["mem"])
    return jax.shard_map(body, mesh=mesh, in_specs=in_specs, out_specs=out_specs, check_vma=False)
```

time: 138 us -> 38.7 us (0.28)
  starting transfers between devices: 45.6 us -> 0 us
  Pallas kernels: 0 us -> 31.2 us
  blocking collectives: 24.3 us -> 0 us
  other arithmetic: 20.6 us -> 0 us
  matrix products: 19.8 us -> 0 us
  local copies, waits for them, and re-layouts: 23.7 us -> 7.26 us
  between operations: 1.64 us -> 0.01 us
    ppermute x14 -> x0, starting transfers between devices: 45.6 us -> none  [from_behind(): lax.ppermute(value, axis, [(source, source + steps) for source in range(f...]
    pallas_call x0 -> x1, Pallas kernels: none -> 31.2 us  [shards(): pl.pallas_call(functools.partial(kernel, devices, ranks), out_shape=jax.S...]
    all_gather x3 -> x0, blocking collectives: 24.3 us -> none  [the longest x2 15.9 us: analyse(): member_piece = lax.all_gather(state_block, 'mem', axis=1, tiled=True)]
    dot_general x44 -> x0, matrix products: 19.8 us -> none  [the longest x12 5.39 us: inverse_root(): jnp.einsum('pij,pjk->pik', middle, inverse_part, precision=exact)]
    gather x17 -> x0, local copies, waits for them, and re-layouts: 10.1 us -> none  [the longest x6 3.38 us: shards(): pulled[chosen_rows]]
    mul x8 -> x0, other arithmetic: 7.86 us -> none  [the longest x6 7.84 us: pick_slots(): rows_here = jnp.sum(owned_flag[..., None] * (wanted - range_start), axis=-2)]
    reduce_sum x15 -> x0, other arithmetic: 5.23 us -> none  [the longest x6 3.87 us: pick_slots(): rows_here = jnp.sum(owned_flag[..., None] * (wanted - range_start), axis=-2)]
    dynamic_update_slice x4 -> x0, local copies, waits for them, and re-layouts: 4.29 us -> none  [analyse(): return lax.dynamic_update_slice_in_dim(output, result, first_slot, 0)]
  transfers between devices with their start and end apart: 14 -> 0, of which waited for: 1 -> 0; matrix products, arithmetic and copies ran while one was open for 19% -> 0% of each run, Pallas kernels for 0% -> 0%
where the time goes in v1:
time: 38.7 us; the launch traced here: 38.4 us
  Pallas kernels  31.2 us (81%)
  local copies, waits for them, and re-layouts  7.26 us (19%)
    pallas_call x1, Pallas kernels, shards(): pl.pallas_call(functools.partial(kernel, devices, ranks), out_shape=jax.S...  31.2 us
    unnamed x6, local copies, waits for them, and re-layouts  5.47 us
    pallas_call x1, local copies, waits for them, and re-layouts, shards(): pl.pallas_call(functools.partial(kernel, devices, ranks), out_shape=jax.S...  1.79 us

profile of v1, /device:TPU:0, one launch (start us, length us, event | category | flops | bytes accessed | tf_op | source)
XLA Modules:
  0.0 38.4 jit_solution(2964848140560275772)
XLA Ops:
  0.0 0.0 copy-start
  0.0 1.4 %copy.12.weight_ref = f32[14,7]{1,0:T(8,128)} copy(f32[14,7]{0,1:T(8,128)} %param.14) | data formatting | bytes 784 | tf_op args[4]
  1.4 0.0 copy-done
  1.4 0.7 %copy.11.region_ref = s32[14,7]{1,0:T(8,128)} copy(s32[14,7]{0,1:T(8,128)S(1)} %copy-done) | data formatting | bytes 784 | tf_op args[9]
  2.1 1.5 %copy.14.obs_ref = bf16[14,20,128]{2,1,0:T(8,128)(2,1)} copy(bf16[14,20,128]{2,0,1:T(8,128)(2,1)} %param.11) | data formatting | bytes 143360 | tf_op args[1]
  3.6 1.9 %copy.13.back_ref = bf16[14,20,512]{2,1,0:T(8,128)(2,1)} copy(bf16[14,20,512]{2,0,1:T(8,128)(2,1)} %param.10) | data formatting | bytes 573440 | tf_op args[0]
  5.5 31.2 %shard_map.100 = bf16[14,20,512]{2,1,0:T(8,128)(2,1)} custom-call(s32[9]{0:T(128)} %old_ref.1, s32[9]{0:T(128)} %new_ref.1, s32[14]{0:T(128)} %count_ref.1, s32[8,12]{1,0:T(8,128)} %halo_ref.1, s32[14,7]{1,0:T(8,128)} %copy.11.region_ref, f32[14,7]{1,0:T(8,128)} %copy.12.weight_ref, bf16[14,20,512]{2,1,0:T(8,128)(2,1)} %copy.13.back_ref, ...), custom_call_target="tpu_custom_call" | custom-call | flops 100000000 | bytes 10000000 | tf_op jit(solution)/shard_map/pallas_call | solution.py:350
  36.7 1.8 %copy.15 = bf16[14,20,512]{2,0,1:T(8,128)(2,1)} copy(bf16[14,20,512]{2,1,0:T(8,128)(2,1)} %shard_map.100) | data formatting | bytes 573440 | tf_op jit(solution)/shard_map/pallas_call | solution.py:350
Async XLA Ops:
  0.0 1.4 %copy-start = (s32[14,7]{0,1:T(8,128)S(1)}, s32[14,7]{0,1:T(8,128)}, u32[]{:S(2)}) copy-start(s32[14,7]{0,1:T(8,128)} %param.19) | copy-start | bytes 1180

commit v2 on v1

--- a/solution.py
+++ b/solution.py
@@ -16,7 +16,7 @@
 NS_ITERS = 6
 LIVE_MAX = TILE_MEAN + MOVE
 INFLATION = 1.1
-PAD = 32
+PAD = 24
 MESH = pl.DeviceIdType.MESH
 F32 = jnp.float32
 BF16 = jnp.bfloat16
@@ -53,6 +53,7 @@
     prec_ref,
     out_ref,
     mine,
+    back_t,
     table,
     stage,
     arrived,
@@ -77,7 +78,7 @@
     t_send,
     t_recv,
 ):
-    capacity, members, width = back_ref.shape
+    members, capacity, width = back_ref.shape
     obs_slots = obs_ref.shape[2]
     ensemble = members * ranks
     full = PAD * ranks
@@ -103,11 +104,12 @@
     row_id = lax.broadcasted_iota(jnp.int32, (PAD, obs_slots), 0)
     lane_id = lax.broadcasted_iota(jnp.int32, (1, obs_slots), 1)
 
+    obs_all = obs_ref[...].astype(F32)
     for s in range(LIVE_MAX):
         live = (lane_id < count_ref[s]).astype(F32)
         root = jnp.sqrt(prec_ref[s : s + 1, :] * live)
         pulled = root * innov_ref[s : s + 1, :]
-        rows = obs_ref[s].astype(F32) * root
+        rows = obs_all[:, s, :] * root
         fill = jnp.zeros((PAD - members, obs_slots), F32)
         block = jnp.concatenate([rows, fill], axis=0)
         block = jnp.where(row_id == members, pulled, block).astype(BF16)
@@ -125,10 +127,6 @@
             index = jnp.clip(index, 0, LIVE_MAX - 1)
             stage[k, c] = mine[index]
 
-    old_count = old_end - old_start
-    for c in range(MOVE):
-        mig_out[0, c] = back_ref[jnp.clip(c, 0, capacity - 1)]
-        mig_out[1, c] = back_ref[jnp.clip(old_count - MOVE + c, 0, capacity - 1)]
     for s in range(LIVE_MAX):
         states[s, rank] = jnp.zeros((PAD, width), BF16)
 
@@ -163,6 +161,43 @@
         def _(copy=copy):
             copy.start()
 
+    own_rows = pl.ds(0, LIVE_MAX)
+    far_rows = pl.ds(LIVE_MAX, halo_count)
+    pair = rank + 1 - 2 * lax.rem(rank, 2)
+    half_ranks = ranks // 2
+
+    def gather(piece, send, recv):
+        here = piece(rank)
+        direct = [remote(here, here, send.at[0], recv.at[0], (me, pair))]
+        passed = []
+        for j in range(1, half_ranks):
+            ahead = lax.rem(rank + 2 * j, ranks)
+            behind = piece(lax.rem(rank + ranks - 2 * j, ranks))
+            direct.append(remote(here, here, send.at[j], recv.at[j], (me, ahead)))
+            k = half_ranks + j - 1
+            passed.append(remote(behind, behind, send.at[k], recv.at[k], (me, pair)))
+        return direct, passed
+
+    def start(copies):
+        for copy in copies:
+            copy.start()
+
+    def arrive(copies):
+        for copy in copies:
+            copy.wait_recv()
+
+    own_copies, own_passed = gather(lambda r: table.at[own_rows, r], own_send, own_recv)
+    far_copies, far_passed = gather(lambda r: table.at[far_rows, r], far_send, far_recv)
+    state_copies, state_passed = gather(lambda r: states.at[:, r], state_send, state_recv)
+    start(own_copies[::-1])
+
+    back_all = back_ref[...].astype(F32)
+    for s in range(capacity):
+        back_t[s] = back_all[:, s, :].astype(BF16)
+    old_count = old_end - old_start
+    for c in range(MOVE):
+        mig_out[0, c] = back_t[jnp.clip(c, 0, capacity - 1)]
+        mig_out[1, c] = back_t[jnp.clip(old_count - MOVE + c, 0, capacity - 1)]
     mig_copies = []
     for side, offset in ((0, -1), (1, 1)):
         target = me + offset
@@ -175,19 +210,6 @@
         @pl.when((target >= 0) & (target < devices))
         def _(copy=copy):
             copy.start()
-
-    own_rows = pl.ds(0, LIVE_MAX)
-    far_rows = pl.ds(LIVE_MAX, halo_count)
-    own_copies, far_copies, state_copies = [], [], []
-    for j, peer in enumerate(peers):
-        own = table.at[own_rows, rank]
-        own_copies.append(remote(own, own, own_send.at[j], own_recv.at[j], (me, peer)))
-        far = table.at[far_rows, rank]
-        far_copies.append(remote(far, far, far_send.at[j], far_recv.at[j], (me, peer)))
-        piece = states.at[:, rank]
-        state_copies.append(remote(piece, piece, state_send.at[j], state_recv.at[j], (me, peer)))
-    for copy in own_copies:
-        copy.start()
 
     for k, offset in enumerate(OFFSETS):
         back_slot = len(OFFSETS) - 1 - k
@@ -207,8 +229,7 @@
             owner = jnp.where(held & inside, k, owner)
         for c in range(HCAP):
             table[LIVE_MAX + g * HCAP + c, rank] = arrived[owner, c]
-    for copy in far_copies:
-        copy.start()
+    start(far_copies[::-1])
 
     for side, offset in ((0, -1), (1, 1)):
         source = me - offset
@@ -220,17 +241,17 @@
     for s in range(LIVE_MAX):
         position = new_start + s
         left = mig_in[0, jnp.clip(position - old_start + MOVE, 0, MOVE - 1)]
-        own = back_ref[jnp.clip(position - old_start, 0, capacity - 1)]
+        own = back_t[jnp.clip(position - old_start, 0, capacity - 1)]
         right = mig_in[1, jnp.clip(position - old_end, 0, MOVE - 1)]
         row = jnp.where(position < old_start, left, jnp.where(position < old_end, own, right))
         states[s, rank, :members] = row
-    for copy in state_copies:
-        copy.start()
-
-    for copy in own_copies:
-        copy.wait_recv()
-    for copy in far_copies:
-        copy.wait_recv()
+    start(state_copies[::-1])
+
+    arrive(own_copies[1:])
+    start(own_passed)
+    arrive(far_copies[1:])
+    start(far_passed)
+    arrive(own_copies[:1] + own_passed + far_copies[:1] + far_passed)
 
     grid_row = lax.broadcasted_iota(jnp.int32, (full, full), 0)
     grid_col = lax.broadcasted_iota(jnp.int32, (full, full), 1)
@@ -241,7 +262,7 @@
     line = lax.broadcasted_iota(jnp.int32, (1, full), 1)
     live_line = lax.rem(line, PAD) < members
     shift = (ensemble - 1) / INFLATION
-    entries = region_ref.shape[1] + 1
+    entries = region_ref.shape[0] + 1
 
     norms, pulls = [], []
     for b in range(per_rank):
@@ -251,14 +272,14 @@
             if e == 0:
                 index = slot
             else:
-                named = region_ref[slot, e - 1]
+                named = region_ref[e - 1, slot]
                 index = jnp.where(named < capacity, named, named - capacity + LIVE_MAX)
             index = jnp.clip(index, 0, LIVE_MAX + halo_count - 1)
             block = table[index].reshape(full, obs_slots)
             product = lax.dot_general(
                 block, block, (((1,), (1,)), ((), ())), preferred_element_type=F32
             )
-            gram += product if e == 0 else weight_ref[slot, e - 1] * product
+            gram += product if e == 0 else weight_ref[e - 1, slot] * product
         pulls.append(jnp.where(live_line, gram[members : members + 1, :], 0.0))
         system = jnp.where(live_row & live_col, gram, 0.0) + shift * live_unit
         total = jnp.sum(jnp.sum(system * system, axis=1, keepdims=True), axis=0, keepdims=True)
@@ -300,10 +321,9 @@
         copy.start()
     t_in[rank] = t_out[:, rank]
 
-    for copy in state_copies:
-        copy.wait_recv()
-    for copy in t_copies:
-        copy.wait_recv()
+    arrive(state_copies[1:])
+    start(state_passed)
+    arrive(t_copies + state_copies[:1] + state_passed)
 
     piece_row = lax.broadcasted_iota(jnp.int32, (PAD, full), 0)
     for s in range(LIVE_MAX):
@@ -332,7 +352,8 @@
         def _(copy=mig_copies[side]):
             copy.wait_send()
 
-    for copy in own_copies + far_copies + state_copies + t_copies:
+    gathers = own_copies + own_passed + far_copies + far_passed + state_copies + state_passed
+    for copy in gathers + t_copies:
         copy.wait_send()
 
 
@@ -354,6 +375,7 @@
         out_specs=vmem,
         scratch_shapes=[
             pltpu.VMEM((LIVE_MAX, PAD, obs_slots), BF16),
+            pltpu.VMEM((capacity, members, width), BF16),
             pltpu.VMEM((LIVE_MAX + halo_count, ranks, PAD, obs_slots), BF16),
             pltpu.VMEM((count, HCAP, PAD, obs_slots), BF16),
             pltpu.VMEM((count, HCAP, PAD, obs_slots), BF16),
@@ -380,8 +402,8 @@
         ],
         compiler_params=pltpu.CompilerParams(collective_id=0, has_side_effects=True),
         cost_estimate=pl.CostEstimate(flops=10**8, bytes_accessed=10**7, transcendentals=0),
-    )(old_split, new_split, obs_count, halo_tiles, region_list, loc_weight, background, obs_ens,
-      innovation, precision)
+    )(old_split, new_split, obs_count, halo_tiles, region_list.T, loc_weight.T,
+      jnp.swapaxes(background, 0, 1), jnp.swapaxes(obs_ens, 0, 1), innovation, precision)
 
 
 def solution(mesh):

time: 38.7 us -> 24.6 us (0.64)
  Pallas kernels: 31.2 us -> 22.6 us
  local copies, waits for them, and re-layouts: 7.26 us -> 1.79 us
    pallas_call x1, Pallas kernels: 31.2 us -> 22.6 us  [shards(): pl.pallas_call(functools.partial(kernel, devices, ranks), out_shape=jax.S...]
    unnamed x6 -> x0, local copies, waits for them, and re-layouts: 5.47 us -> none
where the time goes in v2:
time: 24.6 us; the launch traced here: 24.4 us
  Pallas kernels  22.6 us (92%)
  local copies, waits for them, and re-layouts  1.79 us (7%)
    pallas_call x1, Pallas kernels, shards(): pl.pallas_call(functools.partial(kernel, devices, ranks), out_shape=jax.S...  22.6 us
    pallas_call x1, local copies, waits for them, and re-layouts, shards(): pl.pallas_call(functools.partial(kernel, devices, ranks), out_shape=jax.S...  1.79 us

profile of v2, /device:TPU:0, one launch (start us, length us, event | category | flops | bytes accessed | tf_op | source)
XLA Modules:
  0.0 24.4 jit_solution(4880616280085637036)
XLA Ops:
  0.0 22.6 %shard_map.100 = bf16[14,20,512]{2,1,0:T(8,128)(2,1)} custom-call(s32[9]{0:T(128)} %old_ref.1, s32[9]{0:T(128)} %new_ref.1, s32[14]{0:T(128)} %count_ref.1, s32[8,12]{1,0:T(8,128)} %halo_ref.1, s32[7,14]{1,0:T(8,128)} %bitcast.6, f32[7,14]{1,0:T(8,128)} %bitcast.7, bf16[20,14,512]{2,1,0:T(8,128)(2,1)} %bitcast.4, bf16[20,14,128]{2,1,0:T(8,128)(2,1)} %bitcast.5, ...), custom_call_target="tpu_custom_call" | custom-call | flops 100000000 | bytes 10000000 | tf_op jit(solution)/shard_map/pallas_call | solution.py:371
  22.6 1.8 %copy.11 = bf16[14,20,512]{2,0,1:T(8,128)(2,1)} copy(bf16[14,20,512]{2,1,0:T(8,128)(2,1)} %shard_map.100) | data formatting | bytes 573440 | tf_op jit(solution)/shard_map/pallas_call | solution.py:371

commit v3 on v2

--- a/solution.py
+++ b/solution.py
@@ -14,6 +14,7 @@
 HPEER = 3
 HCAP = 4
 NS_ITERS = 6
+LIVE_MIN = TILE_MEAN - MOVE
 LIVE_MAX = TILE_MEAN + MOVE
 INFLATION = 1.1
 PAD = 24
@@ -35,7 +36,9 @@
 def dot3(a, b):
     ah, al = a
     bh, bl = b
-    return dot(ah, bh) + (dot(ah, bl) + dot(al, bh))
+    rows = ah.shape[0]
+    both = dot(jnp.concatenate([ah, al], axis=0), bh)
+    return both[:rows] + (dot(ah, bl) + both[rows:])
 
 
 def kernel(
@@ -53,6 +56,7 @@
     prec_ref,
     out_ref,
     mine,
+    out_t,
     back_t,
     table,
     stage,
@@ -128,7 +132,7 @@
             stage[k, c] = mine[index]
 
     for s in range(LIVE_MAX):
-        states[s, rank] = jnp.zeros((PAD, width), BF16)
+        states[s, rank, members:] = jnp.zeros((PAD - members, width), BF16)
 
     signals = ranks - 1
     for offset in OFFSETS:
@@ -188,12 +192,25 @@
 
     own_copies, own_passed = gather(lambda r: table.at[own_rows, r], own_send, own_recv)
     far_copies, far_passed = gather(lambda r: table.at[far_rows, r], far_send, far_recv)
-    state_copies, state_passed = gather(lambda r: states.at[:, r], state_send, state_recv)
+    sure = LIVE_MIN - 2 * MOVE
+    chunks = ((MOVE, sure), (0, MOVE), (MOVE + sure, LIVE_MAX - MOVE - sure))
+    pieces = [
+        gather(
+            lambda r, a=a, c=c: states.at[pl.ds(a, c), r],
+            state_send.at[i],
+            state_recv.at[i],
+        )
+        for i, (a, c) in enumerate(chunks)
+    ]
+    state_copies, state_passed = pieces[1][0] + pieces[2][0], pieces[1][1] + pieces[2][1]
     start(own_copies[::-1])
 
     back_all = back_ref[...].astype(F32)
     for s in range(capacity):
         back_t[s] = back_all[:, s, :].astype(BF16)
+    for s in range(MOVE, MOVE + sure):
+        own = back_t[jnp.clip(new_start + s - old_start, 0, capacity - 1)]
+        states[s, rank, :members] = own
     old_count = old_end - old_start
     for c in range(MOVE):
         mig_out[0, c] = back_t[jnp.clip(c, 0, capacity - 1)]
@@ -211,6 +228,8 @@
         def _(copy=copy):
             copy.start()
 
+    start(pieces[0][0][::-1])
+
     for k, offset in enumerate(OFFSETS):
         back_slot = len(OFFSETS) - 1 - k
         source = me + OFFSETS[back_slot]
@@ -238,7 +257,7 @@
         def _(copy=mig_copies[side]):
             copy.wait_recv()
 
-    for s in range(LIVE_MAX):
+    for s in list(range(MOVE)) + list(range(MOVE + sure, LIVE_MAX)):
         position = new_start + s
         left = mig_in[0, jnp.clip(position - old_start + MOVE, 0, MOVE - 1)]
         own = back_t[jnp.clip(position - old_start, 0, capacity - 1)]
@@ -251,6 +270,8 @@
     start(own_passed)
     arrive(far_copies[1:])
     start(far_passed)
+    arrive(pieces[0][0][1:])
+    start(pieces[0][1])
     arrive(own_copies[:1] + own_passed + far_copies[:1] + far_passed)
 
     grid_row = lax.broadcasted_iota(jnp.int32, (full, full), 0)
@@ -305,7 +326,7 @@
         middle = cut(1.5 * unit - 0.5 * dot3(z, cut(y_s[b])))
         inverse = dot3(middle, z)
         parts = cut(inverse)
-        pull = jnp.broadcast_to(pulls[b], (8, full))
+        pull = jnp.broadcast_to(pulls[b], (16, full))
         half = dot3(cut(pull), parts)
         shift_row = dot3(cut(half), parts)[:1] / norms[b]
         spread = math.sqrt(ensemble - 1) * lax.rsqrt(norms[b])
@@ -321,10 +342,14 @@
         copy.start()
     t_in[rank] = t_out[:, rank]
 
-    arrive(state_copies[1:])
-    start(state_passed)
-    arrive(t_copies + state_copies[:1] + state_passed)
-
+    for direct, passed in pieces[1:]:
+        arrive(direct[1:])
+        start(passed)
+    arrive(t_copies + pieces[0][0][:1] + pieces[0][1])
+    for direct, passed in pieces[1:]:
+        arrive(direct[:1] + passed)
+
+    values = []
     piece_row = lax.broadcasted_iota(jnp.int32, (PAD, full), 0)
     for s in range(LIVE_MAX):
         weights = t_in[s % ranks, s // ranks]
@@ -334,9 +359,11 @@
         mean = blended[members : members + 1, :] / ensemble
         value = (blended + keep * mean)[:members]
         is_live = new_start + s < new_end
-        out_ref[s] = jnp.where(is_live, value, 0.0).astype(BF16)
-    for s in range(LIVE_MAX, capacity):
-        out_ref[s] = jnp.zeros((members, width), BF16)
+        values.append(jnp.where(is_live, value, 0.0))
+    values += [jnp.zeros((members, width), F32)] * (capacity - LIVE_MAX)
+    for s, value in enumerate(values):
+        out_t[:, s, :] = value
+    out_ref[...] = out_t[...].astype(BF16)
 
     for k, offset in enumerate(OFFSETS):
         target = me + offset
@@ -352,7 +379,8 @@
         def _(copy=mig_copies[side]):
             copy.wait_send()
 
-    gathers = own_copies + own_passed + far_copies + far_passed + state_copies + state_passed
+    gathers = own_copies + own_passed + far_copies + far_passed + pieces[0][0] + pieces[0][1]
+    gathers += state_copies + state_passed
     for copy in gathers + t_copies:
         copy.wait_send()
 
@@ -368,13 +396,14 @@
     vmem = pl.BlockSpec(memory_space=pltpu.VMEM)
     count = len(OFFSETS)
     dma = pltpu.SemaphoreType.DMA
-    return pl.pallas_call(
+    result = pl.pallas_call(
         functools.partial(kernel, devices, ranks),
-        out_shape=jax.ShapeDtypeStruct((capacity, members, width), BF16),
+        out_shape=jax.ShapeDtypeStruct((members, capacity, width), BF16),
         in_specs=[smem] * 6 + [vmem] * 4,
         out_specs=vmem,
         scratch_shapes=[
             pltpu.VMEM((LIVE_MAX, PAD, obs_slots), BF16),
+            pltpu.VMEM((members, capacity, width), F32),
             pltpu.VMEM((capacity, members, width), BF16),
             pltpu.VMEM((LIVE_MAX + halo_count, ranks, PAD, obs_slots), BF16),
             pltpu.VMEM((count, HCAP, PAD, obs_slots), BF16),
@@ -395,8 +424,8 @@
             dma((ranks - 1,)),
             dma((ranks - 1,)),
             dma((ranks - 1,)),
-            dma((ranks - 1,)),
-            dma((ranks - 1,)),
+            dma((3, ranks - 1)),
+            dma((3, ranks - 1)),
             dma((ranks - 1,)),
             dma((ranks - 1,)),
         ],
@@ -404,6 +433,7 @@
         cost_estimate=pl.CostEstimate(flops=10**8, bytes_accessed=10**7, transcendentals=0),
     )(old_split, new_split, obs_count, halo_tiles, region_list.T, loc_weight.T,
       jnp.swapaxes(background, 0, 1), jnp.swapaxes(obs_ens, 0, 1), innovation, precision)
+    return jnp.swapaxes(result, 0, 1)
 
 
 def solution(mesh):

time: 24.6 us -> 24.7 us (level)
    pallas_call x1 -> x0, local copies, waits for them, and re-layouts: 1.79 us -> none  [shards(): pl.pallas_call(functools.partial(kernel, devices, ranks), out_shape=jax.S...]
    unnamed x0 -> x1, local copies, waits for them, and re-layouts: none -> 1.72 us
where the time goes in v3:
time: 24.7 us; the launch traced here: 24.5 us
  Pallas kernels  22.8 us (92%)
  local copies, waits for them, and re-layouts  1.72 us (7%)
    pallas_call x1, Pallas kernels, shards(): pl.pallas_call(functools.partial(kernel, devices, ranks), out_shape=jax.S...  22.8 us
    unnamed x1, local copies, waits for them, and re-layouts  1.72 us

profile of v3, /device:TPU:0, one launch (start us, length us, event | category | flops | bytes accessed | tf_op | source)
XLA Modules:
  0.0 24.5 jit_solution(11406111914447645818)
XLA Ops:
  0.0 22.8 %shard_map.100 = bf16[20,14,512]{2,1,0:T(8,128)(2,1)} custom-call(s32[9]{0:T(128)} %old_ref.1, s32[9]{0:T(128)} %new_ref.1, s32[14]{0:T(128)} %count_ref.1, s32[8,12]{1,0:T(8,128)} %halo_ref.1, s32[7,14]{1,0:T(8,128)} %bitcast.8, f32[7,14]{1,0:T(8,128)} %bitcast.9, bf16[20,14,512]{2,1,0:T(8,128)(2,1)} %bitcast.6, bf16[20,14,128]{2,1,0:T(8,128)(2,1)} %bitcast.7, ...), custom_call_target="tpu_custom_call" | custom-call | flops 100000000 | bytes 10000000 | tf_op jit(solution)/shard_map/pallas_call | solution.py:399
  22.8 1.7 %copy.12 = bf16[14,20,512]{2,0,1:T(8,128)(2,1)} copy(bf16[14,20,512]{2,0,1:T(8,128)(2,1)} %bitcast.5) | data formatting | bytes 573440

commit v4 on v3

--- a/solution.py
+++ b/solution.py
@@ -56,7 +56,6 @@
     prec_ref,
     out_ref,
     mine,
-    out_t,
     back_t,
     table,
     stage,
@@ -349,7 +348,6 @@
     for direct, passed in pieces[1:]:
         arrive(direct[:1] + passed)
 
-    values = []
     piece_row = lax.broadcasted_iota(jnp.int32, (PAD, full), 0)
     for s in range(LIVE_MAX):
         weights = t_in[s % ranks, s // ranks]
@@ -359,11 +357,9 @@
         mean = blended[members : members + 1, :] / ensemble
         value = (blended + keep * mean)[:members]
         is_live = new_start + s < new_end
-        values.append(jnp.where(is_live, value, 0.0))
-    values += [jnp.zeros((members, width), F32)] * (capacity - LIVE_MAX)
-    for s, value in enumerate(values):
-        out_t[:, s, :] = value
-    out_ref[...] = out_t[...].astype(BF16)
+        out_ref[s] = jnp.where(is_live, value, 0.0).astype(BF16)
+    for s in range(LIVE_MAX, capacity):
+        out_ref[s] = jnp.zeros((members, width), BF16)
 
     for k, offset in enumerate(OFFSETS):
         target = me + offset
@@ -396,14 +392,13 @@
     vmem = pl.BlockSpec(memory_space=pltpu.VMEM)
     count = len(OFFSETS)
     dma = pltpu.SemaphoreType.DMA
-    result = pl.pallas_call(
+    return pl.pallas_call(
         functools.partial(kernel, devices, ranks),
-        out_shape=jax.ShapeDtypeStruct((members, capacity, width), BF16),
+        out_shape=jax.ShapeDtypeStruct((capacity, members, width), BF16),
         in_specs=[smem] * 6 + [vmem] * 4,
         out_specs=vmem,
         scratch_shapes=[
             pltpu.VMEM((LIVE_MAX, PAD, obs_slots), BF16),
-            pltpu.VMEM((members, capacity, width), F32),
             pltpu.VMEM((capacity, members, width), BF16),
             pltpu.VMEM((LIVE_MAX + halo_count, ranks, PAD, obs_slots), BF16),
             pltpu.VMEM((count, HCAP, PAD, obs_slots), BF16),
@@ -433,7 +428,6 @@
         cost_estimate=pl.CostEstimate(flops=10**8, bytes_accessed=10**7, transcendentals=0),
     )(old_split, new_split, obs_count, halo_tiles, region_list.T, loc_weight.T,
       jnp.swapaxes(background, 0, 1), jnp.swapaxes(obs_ens, 0, 1), innovation, precision)
-    return jnp.swapaxes(result, 0, 1)
 
 
 def solution(mesh):

time: 24.7 us -> 24.7 us (level)
    pallas_call x0 -> x1, local copies, waits for them, and re-layouts: none -> 1.79 us  [shards(): pl.pallas_call(functools.partial(kernel, devices, ranks), out_shape=jax.S...]
    unnamed x1 -> x0, local copies, waits for them, and re-layouts: 1.72 us -> none
where the time goes in v4:
time: 24.7 us; the launch traced here: 24.5 us
  Pallas kernels  22.7 us (92%)
  local copies, waits for them, and re-layouts  1.79 us (7%)
    pallas_call x1, Pallas kernels, shards(): pl.pallas_call(functools.partial(kernel, devices, ranks), out_shape=jax.S...  22.7 us
    pallas_call x1, local copies, waits for them, and re-layouts, shards(): pl.pallas_call(functools.partial(kernel, devices, ranks), out_shape=jax.S...  1.79 us

profile of v4, /device:TPU:0, one launch (start us, length us, event | category | flops | bytes accessed | tf_op | source)
XLA Modules:
  0.0 24.5 jit_solution(3265533405381397153)
XLA Ops:
  0.0 22.7 %shard_map.100 = bf16[14,20,512]{2,1,0:T(8,128)(2,1)} custom-call(s32[9]{0:T(128)} %old_ref.1, s32[9]{0:T(128)} %new_ref.1, s32[14]{0:T(128)} %count_ref.1, s32[8,12]{1,0:T(8,128)} %halo_ref.1, s32[7,14]{1,0:T(8,128)} %bitcast.6, f32[7,14]{1,0:T(8,128)} %bitcast.7, bf16[20,14,512]{2,1,0:T(8,128)(2,1)} %bitcast.4, bf16[20,14,128]{2,1,0:T(8,128)(2,1)} %bitcast.5, ...), custom_call_target="tpu_custom_call" | custom-call | flops 100000000 | bytes 10000000 | tf_op jit(solution)/shard_map/pallas_call | solution.py:395
  22.7 1.8 %copy.11 = bf16[14,20,512]{2,0,1:T(8,128)(2,1)} copy(bf16[14,20,512]{2,1,0:T(8,128)(2,1)} %shard_map.100) | data formatting | bytes 573440 | tf_op jit(solution)/shard_map/pallas_call | solution.py:395
